TPU v7x, 32 devices: a whole 2x2x4 slice. The times are simulated.
32 devices in a mesh: groups: 2 (over y), patch: 2 (over x), cfg: 2 (over core), head: 4 (over z).
Axes of the slice: x: 2, y: 2, z: 4, core: 2. Of those that a mesh axis runs over, the one named last changes fastest.
Arguments:
- img_hidden: bfloat16 [2, 1024, 3072], P('cfg', ('groups', 'patch')), parts along dimension 1, may hold values from -40 to 40
- txt_hidden: bfloat16 [2, 64, 3072], P('cfg', ('groups', 'patch')), parts along dimension 1, may hold values from -6 to 6
- modulation: float32 [4, 3, 3072], P(('groups', 'cfg')), parts along dimension 0, may hold values from -4 to 4
- w_qkv: bfloat16 [3072, 3, 1536], P(None, None, 'head'), may hold values from -0.109375 to 0.109375
- q_gain: float32 [128], replicated, may hold values from 1.2 to 2.5
- k_gain: float32 [128], replicated, may hold values from 1.2 to 2.5
- w_out: bfloat16 [1536, 3072], P('head'), may hold values from -0.15625 to 0.15625
- b_out: float32 [3072], replicated, may hold values from -3 to 3
- stale_kv: bfloat16 [2, 2, 1088, 1536], P('cfg', None, ('groups', 'patch'), 'head'), parts along dimension 2, may hold values from -500 to 500
- final_mod: float32 [4, 2, 3072], P(('groups', 'cfg')), parts along dimension 0, may hold values from -3 to 3
- w_final: bfloat16 [3072, 64], replicated, may hold values from -0.109375 to 0.109375
- b_final: float32 [64], replicated, may hold values from -3 to 3
- latent: float32 [1024, 64], P(('groups', 'patch', 'cfg', 'head')), parts along dimension 0, may hold values from -6 to 6
- prev_denoised: float32 [1024, 64], P(('groups', 'patch', 'cfg', 'head')), parts along dimension 0, may hold values from -24 to 24
- guidance: float32 [2], P('groups'), parts along dimension 0, may hold values from 2 to 5
- step_index: int32 [1], replicated, may hold values from 14 to 21
- step_count: int32 [1], replicated, may hold values from 24 to 27
Outputs:
- fresh_kv: bfloat16 [2, 2, 1088, 1536], P('cfg', None, ('groups', 'patch'), 'head'), parts along dimension 2
- next_latent: float32 [1024, 64], P(('groups', 'patch', 'cfg', 'head')), parts along dimension 0
- denoised: float32 [1024, 64], P(('groups', 'patch', 'cfg', 'head')), parts along dimension 0
There are 2 independent parts, one for each index of `groups`. A program takes and returns all parts, laid end to end along the dimension named above; an argument that names none is the same for every part. Nothing has to cross between parts.
All inputs are finite; a program needn't handle non-finite values.
Results may differ from a plain program's by a relative error of at most 0.0075.
The roundings to bfloat16 on the way count: a program that leaves them out, or rounds other values in their place, can miss the bound.
Values may be sent and summed in bfloat16 or wider, within the bound.
A program may use at most 128 MiB of HBM per device.

v0:
```python
import functools
import math

import jax
import jax.numpy as jnp
from jax import lax
from jax.experimental import pallas as pl
from jax.experimental.pallas import tpu as pltpu
from jax.sharding import PartitionSpec as P

HD = 128
GRID_W = 128
CHUNKS = 6
LN_ROWS = 16
LN_UNROLL = 4
VMEM_MAIN = 67043328

epsilon = 1e-06
time_shift = 3.0
MESH = pl.DeviceIdType.MESH


def normed(values):
    centered = values - jnp.mean(values, axis=-1, keepdims=True)
    variance = jnp.mean(centered * centered, axis=-1, keepdims=True)
    return centered * lax.rsqrt(variance + epsilon)


def noise_level(index, count):
    frac = 1.0 - index / count
    lift = math.exp(time_shift)
    return lift * frac / (lift * frac + 1.0 - frac)


def log_ratio(sigma_val):
    return jnp.log(1.0 - sigma_val) - jnp.log(sigma_val)


def rotation_tables(cos_ref, sin_ref, txt_rows, first_pos):
    shape = cos_ref.shape
    quarter = HD // 4
    rows = lax.broadcasted_iota(jnp.int32, shape, 0)
    lanes = lax.broadcasted_iota(jnp.int32, shape, 1)
    pos = jnp.where(rows >= txt_rows, rows - txt_rows + first_pos, 0)
    place = jnp.where(lanes < 2 * quarter, pos // GRID_W, pos % GRID_W).astype(jnp.float32)
    step = (lanes % quarter).astype(jnp.float32)
    angle = place * jnp.exp(step * (-math.log(10000.0) / quarter))
    sine = jnp.sin(angle)
    cos_ref[...] = jnp.cos(angle)
    sin_ref[...] = jnp.where(lanes % (2 * quarter) < quarter, -sine, sine)


def rotated(values, gain, cosine, sine):
    quarter = HD // 4
    v = values * lax.rsqrt(jnp.mean(values * values, axis=-1, keepdims=True) + epsilon) * gain
    lanes = lax.broadcasted_iota(jnp.int32, v.shape, 1)
    swapped = jnp.where(
        lanes % (2 * quarter) < quarter,
        pltpu.roll(v, HD - quarter, 1),
        pltpu.roll(v, quarter, 1),
    )
    return (v * cosine + swapped * sine).astype(jnp.bfloat16)


def kernel(
    n_patch,
    hid, txt, mod, w_qkv, q_gain, k_gain, w_out, b_out, stale, fmod, w_fin, b_fin, lat, prev,
    guidance, step_index, step_count,
    fresh_s, step_o,
    hid_v, txt_v, mod_v, w_v, qg_v, kg_v, wo_v, bo_v, fmod_v, wf_v, bf_v, lat_v, prev_v,
    modded, proj, cos_s, sin_s, q_s, kv_s, m_s, l_s, acc_s, attn_s,
    part, got1, fwd, got2, mixed, vel_s, vel_r,
    loc_sem, kv_send, kv_recv, s1_send, s1_recv, s2_send, s2_recv, v_send, v_recv,
):
    patch = lax.axis_index("patch")
    cfg = lax.axis_index("cfg")
    head = lax.axis_index("head")
    head_lo, head_hi = lax.rem(head, 2), lax.div(head, 2)
    flip1 = head_hi * 2 + (1 - head_lo)
    flip3 = 3 - head
    other_cfg = 1 - cfg
    img_rows, d = hid_v.shape
    txt_rows = txt_v.shape[0]
    kv_rows = img_rows + txt_rows
    head_width = wo_v.shape[0]
    heads = head_width // HD
    out_rows = lat_v.shape[0]
    own_rows = 2 * out_rows
    cols = d // CHUNKS

    pairs = [
        (mod, mod_v), (txt, txt_v), (hid, hid_v),
        (w_qkv.at[1], w_v.at[1]), (w_qkv.at[2], w_v.at[2]), (w_qkv.at[0], w_v.at[0]),
        (k_gain, kg_v), (q_gain, qg_v), (w_out, wo_v), (b_out, bo_v),
        (fmod, fmod_v), (w_fin, wf_v), (b_fin, bf_v), (lat, lat_v), (prev, prev_v),
    ]
    local = [pltpu.make_async_copy(s, t, loc_sem.at[i]) for i, (s, t) in enumerate(pairs)]
    for copy in local:
        copy.start()

    barrier = pltpu.get_barrier_semaphore()
    for j in range(1, n_patch):
        pl.semaphore_signal(
            barrier, inc=1, device_id={"patch": lax.rem(patch + j, n_patch)}, device_id_type=MESH
        )
    pl.semaphore_signal(barrier, inc=1, device_id={"head": flip1}, device_id_type=MESH)
    pl.semaphore_signal(barrier, inc=1, device_id={"head": flip3}, device_id_type=MESH)
    pl.semaphore_signal(barrier, inc=1, device_id={"cfg": other_cfg}, device_id_type=MESH)
    pl.semaphore_wait(barrier, n_patch + 2)

    kv_copies = []
    for which in range(2):
        for j in range(1, n_patch):
            copy = pltpu.make_async_remote_copy(
                src_ref=stale.at[which],
                dst_ref=kv_s.at[j - 1, which],
                send_sem=kv_send.at[j - 1, which],
                recv_sem=kv_recv.at[j - 1, which],
                device_id={"patch": lax.rem(patch + j, n_patch)},
                device_id_type=MESH,
            )
            copy.start()
            kv_copies.append(copy)

    rotation_tables(cos_s, sin_s, txt_rows, patch * img_rows)

    for copy in local[:3]:
        copy.wait()

    def modulate(values):
        out = normed(values.astype(jnp.float32)) * (1.0 + mod_v[1]) + mod_v[0]
        return out.astype(jnp.bfloat16)

    modded[pl.ds(0, txt_rows), :] = modulate(txt_v[...])

    def ln_step(i, carry):
        at = pl.multiple_of(i * LN_ROWS, LN_ROWS)
        modded[pl.ds(at + txt_rows, LN_ROWS), :] = modulate(hid_v[pl.ds(at, LN_ROWS), :])
        return carry

    lax.fori_loop(0, img_rows // LN_ROWS, ln_step, 0, unroll=LN_UNROLL)

    local[3].wait()
    local[6].wait()
    proj[...] = jnp.dot(modded[...], w_v[1], preferred_element_type=jnp.float32)
    for hh in range(heads):
        at = pl.ds(hh * HD, HD)
        fresh_s[0, :, at] = rotated(proj[:, at], kg_v[...], cos_s[...], sin_s[...])
    local[4].wait()
    fresh_s[1] = jnp.dot(modded[...], w_v[2], preferred_element_type=jnp.float32).astype(
        jnp.bfloat16
    )
    local[5].wait()
    local[7].wait()
    img_at = pl.ds(txt_rows, img_rows)
    proj[img_at, :] = jnp.dot(modded[img_at, :], w_v[0], preferred_element_type=jnp.float32)
    for hh in range(heads):
        at = pl.ds(hh * HD, HD)
        q_s[:, at] = rotated(proj[img_at, at], qg_v[...], cos_s[img_at, :], sin_s[img_at, :])

    exp_scale = HD ** (-0.5) * math.log2(math.e)

    def scores_of(hh, keys):
        return (
            lax.dot_general(
                q_s[:, pl.ds(hh * HD, HD)],
                keys,
                (((1,), (1,)), ((), ())),
                preferred_element_type=jnp.float32,
            )
            * exp_scale
        )

    for hh in range(heads):
        at = pl.ds(hh * HD, HD)
        scores = scores_of(hh, fresh_s[0, :, at])
        top = jnp.max(scores, axis=-1, keepdims=True)
        expo = jnp.exp2(scores - top)
        m_s[hh] = top
        l_s[hh] = jnp.sum(expo, axis=-1, keepdims=True)
        acc_s[hh] = jnp.dot(
            expo.astype(jnp.bfloat16), fresh_s[1, :, at], preferred_element_type=jnp.float32
        )

    for copy in kv_copies:
        copy.wait_recv()

    def other_block(j):
        for hh in range(heads):
            at = pl.ds(hh * HD, HD)
            scores = scores_of(hh, kv_s[j, 0, :, at])
            old = m_s[hh]
            top = jnp.maximum(old, jnp.max(scores, axis=-1, keepdims=True))
            factor = jnp.exp2(old - top)
            expo = jnp.exp2(scores - top)
            m_s[hh] = top
            l_s[hh] = l_s[hh] * factor + jnp.sum(expo, axis=-1, keepdims=True)
            acc_s[hh] = acc_s[hh] * factor + jnp.dot(
                expo.astype(jnp.bfloat16), kv_s[j, 1, :, at], preferred_element_type=jnp.float32
            )

    if n_patch <= 2:
        for j in range(n_patch - 1):
            other_block(j)
    else:
        lax.fori_loop(0, n_patch - 1, lambda j, c: (other_block(j), c)[1], 0)

    for hh in range(heads):
        at = pl.ds(hh * HD, HD)
        attn = (acc_s[hh] / l_s[hh]).astype(jnp.bfloat16)
        for g in range(4):
            slot = lax.rem(g // 2 + head_hi, 2) * 2 + lax.rem(g % 2 + head_lo, 2)
            for half in range(2):
                first = half * 4 * out_rows + g * out_rows
                to = pl.multiple_of(slot * own_rows + half * out_rows, out_rows)
                attn_s[pl.ds(to, out_rows), at] = attn[first : first + out_rows]

    local[8].wait()
    step1 = []
    for c in range(CHUNKS):
        part[c] = jnp.dot(
            attn_s[...], wo_v[:, pl.ds(c * cols, cols)], preferred_element_type=jnp.float32
        ).astype(jnp.bfloat16)
        first = 1 if c % 2 == 0 else 2
        copy = pltpu.make_async_remote_copy(
            src_ref=part.at[c, pl.ds(first * own_rows, 2 * own_rows)],
            dst_ref=got1.at[c],
            send_sem=s1_send.at[c],
            recv_sem=s1_recv.at[c],
            device_id={"head": flip1 if c % 2 == 0 else flip3},
            device_id_type=MESH,
        )
        copy.start()
        step1.append(copy)

    for copy in local[9:]:
        copy.wait()

    def f32(values):
        return values.astype(jnp.float32)

    step2 = []
    for c in range(CHUNKS):
        step1[c].wait_recv()
        pass_slot, pass_at = (3, own_rows) if c % 2 == 0 else (1, 0)
        fwd[c] = (
            f32(part[c, pl.ds(pass_slot * own_rows, own_rows), :])
            + f32(got1[c, pl.ds(pass_at, own_rows), :])
        ).astype(jnp.bfloat16)
        copy = pltpu.make_async_remote_copy(
            src_ref=fwd.at[c],
            dst_ref=got2.at[c],
            send_sem=s2_send.at[c],
            recv_sem=s2_recv.at[c],
            device_id={"head": flip3 if c % 2 == 0 else flip1},
            device_id_type=MESH,
        )
        copy.start()
        step2.append(copy)

    for c in range(CHUNKS):
        step2[c].wait_recv()
        keep_at = 0 if c % 2 == 0 else own_rows
        at = pl.ds(c * cols, cols)
        projected = (
            f32(part[c, pl.ds(0, own_rows), :])
            + f32(got1[c, pl.ds(keep_at, own_rows), :])
            + f32(got2[c])
        )
        update = mod_v[2, :, at] * (projected + bo_v[:, at])
        for half in range(2):
            first = pl.multiple_of(half * 4 * out_rows + head * out_rows, out_rows)
            rows = pl.ds(half * out_rows, out_rows)
            mixed[rows, at] = (
                f32(hid_v[pl.ds(first, out_rows), at])
                + update[half * out_rows : (half + 1) * out_rows]
            )

    def final_step(i, carry):
        at = pl.ds(pl.multiple_of(i * LN_ROWS, LN_ROWS), LN_ROWS)
        out = normed(mixed[at, :]) * (1.0 + fmod_v[1:2, :]) + fmod_v[0:1, :]
        modded[at, :] = out.astype(jnp.bfloat16)
        return carry

    lax.fori_loop(0, own_rows // LN_ROWS, final_step, 0, unroll=LN_UNROLL)
    velocity = (
        lax.dot_general(
            modded[pl.ds(0, own_rows), :],
            wf_v[...],
            (((1,), (1,)), ((), ())),
            preferred_element_type=jnp.float32,
        )
        + bf_v[...]
    )
    for half in range(2):
        vel_s[half] = velocity[half * out_rows : (half + 1) * out_rows]
    swap = pltpu.make_async_remote_copy(
        src_ref=vel_s.at[other_cfg],
        dst_ref=vel_r,
        send_sem=v_send,
        recv_sem=v_recv,
        device_id={"cfg": other_cfg},
        device_id_type=MESH,
    )
    swap.start()

    ones = jnp.ones(lat_v.shape, jnp.float32)
    index = ones * step_index[0].astype(jnp.float32)
    count = ones * step_count[0].astype(jnp.float32)
    sigma_prev = noise_level(index - 1.0, count)
    sigma_now = noise_level(index, count)
    sigma_next = noise_level(index + 1.0, count)
    step_now = log_ratio(sigma_next) - log_ratio(sigma_now)
    step_prev = log_ratio(sigma_now) - log_ratio(sigma_prev)
    ratio = step_prev / step_now
    shrink = (1.0 - sigma_next) * (jnp.exp(-step_now) - 1.0)
    latent = lat_v[...]
    swap.wait_recv()
    mine, theirs = vel_s[cfg], vel_r[...]
    is_cond = cfg == 0
    cond = jnp.where(is_cond, mine, theirs)
    uncond = jnp.where(is_cond, theirs, mine)
    guided = uncond + guidance[0] * (cond - uncond)
    denoised = latent - sigma_now * guided
    blend = (1.0 + 0.5 / ratio) * denoised - 0.5 / ratio * prev_v[...]
    step_o[1] = denoised
    step_o[0] = sigma_next / sigma_now * latent - shrink * blend

    for copy in kv_copies + step1 + step2 + [swap]:
        copy.wait_send()


def deliver(fresh, stepped, fresh_o, next_o, den_o, fresh_v, step_v, in_sem, out_sem):
    loads = [
        pltpu.make_async_copy(stepped, step_v, in_sem.at[0]),
        pltpu.make_async_copy(fresh, fresh_v, in_sem.at[1]),
    ]
    for copy in loads:
        copy.start()
    pairs = ((step_v.at[0], next_o), (step_v.at[1], den_o), (fresh_v, fresh_o))
    stores = [pltpu.make_async_copy(s, t, out_sem.at[i]) for i, (s, t) in enumerate(pairs)]
    loads[0].wait()
    stores[0].start()
    stores[1].start()
    loads[1].wait()
    stores[2].start()
    for copy in stores:
        copy.wait()


def body(
    n_patch,
    img_hidden, txt_hidden, modulation, w_qkv, q_gain, k_gain, w_out, b_out, stale_kv,
    final_mod, w_final, b_final, latent, prev_denoised, guidance, step_index, step_count,
):
    bf16, f32 = jnp.bfloat16, jnp.float32
    img_rows, d = img_hidden.shape[1:]
    txt_rows = txt_hidden.shape[1]
    kv_rows = img_rows + txt_rows
    head_width = w_out.shape[0]
    heads = head_width // HD
    out_rows, channels = latent.shape
    own_rows = 2 * out_rows
    cols = d // CHUNKS
    args = (
        img_hidden[0],
        txt_hidden[0],
        modulation.transpose(1, 0, 2),
        w_qkv.transpose(1, 0, 2),
        q_gain[None],
        k_gain[None],
        w_out,
        b_out[None],
        stale_kv[0],
        final_mod[0],
        w_final.T,
        b_final[None],
        latent,
        prev_denoised,
    )
    staged = [a for i, a in enumerate(args) if i != 8]
    dma = pltpu.SemaphoreType.DMA
    scratch = [pltpu.VMEM(a.shape, a.dtype) for a in staged] + [
        pltpu.VMEM((kv_rows, d), bf16),
        pltpu.VMEM((kv_rows, head_width), f32),
        pltpu.VMEM((kv_rows, HD), f32),
        pltpu.VMEM((kv_rows, HD), f32),
        pltpu.VMEM((img_rows, head_width), bf16),
        pltpu.VMEM((n_patch - 1, 2, kv_rows, head_width), bf16),
        pltpu.VMEM((heads, img_rows, 1), f32),
        pltpu.VMEM((heads, img_rows, 1), f32),
        pltpu.VMEM((heads, img_rows, HD), f32),
        pltpu.VMEM((img_rows, head_width), bf16),
        pltpu.VMEM((CHUNKS, img_rows, cols), bf16),
        pltpu.VMEM((CHUNKS, 2 * own_rows, cols), bf16),
        pltpu.VMEM((CHUNKS, own_rows, cols), bf16),
        pltpu.VMEM((CHUNKS, own_rows, cols), bf16),
        pltpu.VMEM((own_rows, d), f32),
        pltpu.VMEM((2, out_rows, channels), f32),
        pltpu.VMEM((out_rows, channels), f32),
        dma((15,)),
        dma((n_patch - 1, 2)),
        dma((n_patch - 1, 2)),
        dma((CHUNKS,)),
        dma((CHUNKS,)),
        dma((CHUNKS,)),
        dma((CHUNKS,)),
        dma,
        dma,
    ]
    vmem = pl.BlockSpec(memory_space=pltpu.VMEM)
    smem = pl.BlockSpec(memory_space=pltpu.SMEM)
    anywhere = pl.BlockSpec(memory_space=pl.ANY)
    fresh, stepped = pl.pallas_call(
        functools.partial(kernel, n_patch),
        out_shape=(
            jax.ShapeDtypeStruct((2, kv_rows, head_width), bf16),
            jax.ShapeDtypeStruct((2, out_rows, channels), f32),
        ),
        in_specs=[anywhere] * len(args) + [smem] * 3,
        out_specs=(vmem, vmem),
        scratch_shapes=scratch,
        compiler_params=pltpu.CompilerParams(
            collective_id=0, has_side_effects=True, vmem_limit_bytes=VMEM_MAIN
        ),
    )(*args, guidance, step_index, step_count)
    fresh, next_latent, denoised = pl.pallas_call(
        deliver,
        out_shape=(
            jax.ShapeDtypeStruct(fresh.shape, bf16),
            jax.ShapeDtypeStruct(latent.shape, f32),
            jax.ShapeDtypeStruct(latent.shape, f32),
        ),
        in_specs=[anywhere, anywhere],
        out_specs=(anywhere, anywhere, anywhere),
        scratch_shapes=[
            pltpu.VMEM(fresh.shape, bf16),
            pltpu.VMEM(stepped.shape, f32),
            dma((2,)),
            dma((3,)),
        ],
        compiler_params=pltpu.CompilerParams(vmem_limit_bytes=VMEM_MAIN),
    )(fresh, stepped)
    return fresh[None], next_latent, denoised


def solution(mesh):
    return jax.shard_map(
        functools.partial(body, mesh.shape["patch"]),
        mesh=mesh,
        in_specs=(
            P("cfg", ("groups", "patch"), None),
            P("cfg", ("groups", "patch"), None),
            P(("groups", "cfg"), None, None),
            P(None, None, "head"),
            P(),
            P(),
            P("head", None),
            P(),
            P("cfg", None, ("groups", "patch"), "head"),
            P(("groups", "cfg"), None, None),
            P(),
            P(),
            P(("groups", "patch", "cfg", "head"), None),
            P(("groups", "patch", "cfg", "head"), None),
            P("groups"),
            P(),
            P(),
        ),
        out_specs=(
            P("cfg", None, ("groups", "patch"), "head"),
            P(("groups", "patch", "cfg", "head"), None),
            P(("groups", "patch", "cfg", "head"), None),
        ),
        check_vma=False,
    )
```

profile of v0, /device:TPU:1, one launch (start us, length us, event | category | flops | bytes accessed | tf_op | source)
XLA Modules:
  0.0 50.7 jit_solution(3227861666948473682)
XLA Ops:
  2.6 46.3 %shard_map.184 = (bf16[2,272,384]{2,1,0:T(8,128)(2,1)}, f32[2,32,64]{2,1,0:T(8,128)}) custom-call(bf16[256,3072]{1,0:T(8,128)(2,1)} %bitcast.13, bf16[16,3072]{1,0:T(8,128)(2,1)} %bitcast.16, f32[3,1,3072]{2,1,0:T(1,128)} %bitcast.17, bf16[3,3072,384]{2,1,0:T(8,128)(2,1)} %bitcast.12, f32[1,128]{1,0:T(1,128)} %bitcast.20, f32[1,128]{1,0:T(1,128)} %bitcast.21, ...), custom_call_target="tpu_custom_call" | custom-call | tf_op jit(solution)/shard_map/pallas_call | solution.py:414
  48.9 1.8 %shard_map.185 = (bf16[2,272,384]{2,1,0:T(8,128)(2,1)}, f32[32,64]{1,0:T(8,128)}, f32[32,64]{1,0:T(8,128)}) custom-call(bf16[2,272,384]{2,1,0:T(8,128)(2,1)} %get-tuple-element.8.fresh, f32[2,32,64]{2,1,0:T(8,128)} %get-tuple-element.9.stepped), custom_call_target="tpu_custom_call" | custom-call | tf_op jit(solution)/shard_map/pallas_call | solution.py:427
where the time goes:
time: 51 us; the launch traced here: 50.7 us
  Pallas kernels  48.1 us (94%)
  between operations  2.58 us (5%)
    pallas_call x1, Pallas kernels, body(): pl.pallas_call(functools.partial(kernel, n_patch), out_shape=(jax.ShapeDt...  46.3 us
    pallas_call x1, Pallas kernels, body(): pl.pallas_call(deliver, out_shape=(jax.ShapeDtypeStruct(fresh.shape, bf16...  1.82 us

commit v1 on v0

v1 whole, which is shorter than its diff:
```python
import functools
import math

import jax
import jax.numpy as jnp
from jax import lax
from jax.experimental import pallas as pl
from jax.experimental.pallas import tpu as pltpu
from jax.sharding import PartitionSpec as P

HD = 128
GRID_W = 128
LN_ROWS = 16
LN_UNROLL = 4
THIRDS = 3
PLANE = 8
VMEM_MAIN = 67043328

epsilon = 1e-06
time_shift = 3.0
MESH = pl.DeviceIdType.MESH


def normed(values):
    centered = values - jnp.mean(values, axis=-1, keepdims=True)
    variance = jnp.mean(centered * centered, axis=-1, keepdims=True)
    return centered * lax.rsqrt(variance + epsilon)


def noise_level(index, count):
    frac = 1.0 - index / count
    lift = math.exp(time_shift)
    return lift * frac / (lift * frac + 1.0 - frac)


def log_ratio(sigma_val):
    return jnp.log(1.0 - sigma_val) - jnp.log(sigma_val)


def rotation_tables(cos_ref, sin_ref, txt_rows, first_pos):
    shape = cos_ref.shape
    quarter = HD // 4
    rows = lax.broadcasted_iota(jnp.int32, shape, 0)
    lanes = lax.broadcasted_iota(jnp.int32, shape, 1)
    pos = jnp.where(rows >= txt_rows, rows - txt_rows + first_pos, 0)
    place = jnp.where(lanes < 2 * quarter, pos // GRID_W, pos % GRID_W).astype(jnp.float32)
    step = (lanes % quarter).astype(jnp.float32)
    angle = place * jnp.exp(step * (-math.log(10000.0) / quarter))
    sine = jnp.sin(angle)
    cos_ref[...] = jnp.cos(angle)
    sin_ref[...] = jnp.where(lanes % (2 * quarter) < quarter, -sine, sine)


def rotated(values, gain, cosine, sine):
    quarter = HD // 4
    v = values * lax.rsqrt(jnp.mean(values * values, axis=-1, keepdims=True) + epsilon) * gain
    lanes = lax.broadcasted_iota(jnp.int32, v.shape, 1)
    swapped = jnp.where(
        lanes % (2 * quarter) < quarter,
        pltpu.roll(v, HD - quarter, 1),
        pltpu.roll(v, quarter, 1),
    )
    return (v * cosine + swapped * sine).astype(jnp.bfloat16)


def kernel(
    n_patch,
    hid, txt, mod, w_qkv, q_gain, k_gain, w_out, b_out, stale, fmod, w_fin, b_fin, lat, prev,
    guidance, step_index, step_count,
    fresh_s, step_o,
    hid_v, txt_v, mod_v, w_v, qg_v, kg_v, wo_v, bo_v, fmod_v, wf_v, bf_v, lat_v, prev_v,
    modded, proj, cos_s, sin_s, q_s, kv_s, m_s, l_s, acc_s, attn_s, attn_in,
    w_in, out_acc, hi_s, lo_s, stat_s, vel_s, vel_in, vec_s, vec_in,
    loc_sem, kv_send, kv_recv, wz_send, wz_recv, wx_send, wx_recv, wy_send, wy_recv,
    wc_send, wc_recv, at_send, at_recv, fw_send, v_send, v_recv, u_send, u_recv,
):
    patch = lax.axis_index("patch")
    group = lax.axis_index("groups")
    cfg = lax.axis_index("cfg")
    head = lax.axis_index("head")
    side = lax.div(head, 2)
    third = lax.rem(head, THIRDS)
    is_end = third == 0
    is_mid = third != 0
    mate = 2 * side + 1 - lax.rem(head, 2)
    partners = (mate, 3 - head, lax.rem(head + 2, 4))
    x_bit = lax.rem(patch, 2)
    x_dev = {"patch": patch + 1 - 2 * x_bit}
    y_dev = {"groups": 1 - group}
    c_dev = {"cfg": 1 - cfg}
    img_rows, d = hid_v.shape
    txt_rows = txt_v.shape[0]
    head_width = wo_v.shape[0]
    heads = head_width // HD
    out_rows = lat_v.shape[0]
    half = img_rows // 2
    cols = d // THIRDS
    share = head_width // PLANE
    my_cols = pl.ds(pl.multiple_of(third * cols, HD), cols)
    half_at = pl.ds(pl.multiple_of(side * half, half), half)

    pairs = [
        (mod, mod_v), (txt, txt_v), (hid, hid_v),
        (w_qkv.at[1], w_v.at[1]), (w_qkv.at[2], w_v.at[2]), (w_qkv.at[0], w_v.at[0]),
        (k_gain, kg_v), (q_gain, qg_v), (w_out.at[:, my_cols], wo_v), (b_out, bo_v),
        (fmod, fmod_v), (w_fin.at[:, my_cols], wf_v.at[pl.ds(0, w_fin.shape[0])]),
        (b_fin, bf_v), (lat, lat_v), (prev, prev_v),
    ]
    local = [pltpu.make_async_copy(s, t, loc_sem.at[i]) for i, (s, t) in enumerate(pairs)]
    for copy in local:
        copy.start()

    def remote(source, target, send, recv, device):
        return pltpu.make_async_remote_copy(
            src_ref=source, dst_ref=target, send_sem=send, recv_sem=recv,
            device_id=device, device_id_type=MESH,
        )

    peers = [{"patch": lax.rem(patch + j, n_patch)} for j in range(1, n_patch)] + [y_dev]
    owners = [(dc, dh) for dc in range(2) for dh in range(4)]
    for dc, dh in owners[1:]:
        peers.append({"cfg": lax.rem(cfg + dc, 2), "head": lax.rem(head + dh, 4)})
    barrier = pltpu.get_barrier_semaphore()
    for peer in peers:
        pl.semaphore_signal(barrier, inc=1, device_id=peer, device_id_type=MESH)
    rotation_tables(cos_s, sin_s, txt_rows, patch * img_rows)
    pl.semaphore_wait(barrier, len(peers))

    def kv_copy(j, hh, which):
        return remote(
            stale.at[which, :, pl.ds(hh * HD, HD)], kv_s.at[j - 1, which, hh],
            kv_send.at[j - 1, which, hh], kv_recv.at[j - 1, which, hh],
            {"patch": lax.rem(patch + j, n_patch)},
        )

    for hh in range(heads):
        for which in range(2):
            for j in range(1, n_patch):
                kv_copy(j, hh, which).start()

    def unit(x, y, c):
        one = 1 - cfg if c else cfg
        two = 1 - group if y else group
        three = 1 - x_bit if x else x_bit
        return pl.ds(pl.multiple_of((one * 4 + two * 2 + three) * share, 16), share)

    own = unit(0, 0, 0)

    def w_over_z(r):
        to = partners[r]
        at = pl.ds(pl.multiple_of(lax.rem(to, THIRDS) * cols, HD), cols)
        return remote(
            w_out.at[own, at], w_in.at[r, own], wz_send.at[r], wz_recv.at[r], {"head": to}
        )

    def w_over_x(r):
        at = w_in.at[r, own]
        return remote(at, at, wx_send.at[r], wx_recv.at[r], x_dev)

    def w_over_y(r, k):
        at = w_in.at[r, unit(k, 0, 0)]
        return remote(at, at, wy_send.at[r, k], wy_recv.at[r, k], y_dev)

    def w_over_c(r, k):
        at = w_in.at[r, unit(k % 2, k // 2, 0)]
        return remote(at, at, wc_send.at[r, k], wc_recv.at[r, k], c_dev)

    order = (0, 2, 1)
    for r in order:
        w_over_z(r).start()

    def w_landed(r):
        w_over_z(r).wait_recv()
        w_over_x(r).start()
        w_over_y(r, 0).start()
        w_over_c(r, 0).start()

    for copy in local[:3]:
        copy.wait()

    def modulate(values):
        out = normed(values.astype(jnp.float32)) * (1.0 + mod_v[1]) + mod_v[0]
        return out.astype(jnp.bfloat16)

    modded[pl.ds(0, txt_rows), :] = modulate(txt_v[...])

    def ln_step(i, carry):
        at = pl.multiple_of(i * LN_ROWS, LN_ROWS)
        modded[pl.ds(at + txt_rows, LN_ROWS), :] = modulate(hid_v[pl.ds(at, LN_ROWS), :])
        return carry

    lax.fori_loop(0, img_rows // LN_ROWS, ln_step, 0, unroll=LN_UNROLL)

    local[3].wait()
    local[6].wait()
    proj[...] = jnp.dot(modded[...], w_v[1], preferred_element_type=jnp.float32)
    for hh in range(heads):
        at = pl.ds(hh * HD, HD)
        fresh_s[0, :, at] = rotated(proj[:, at], kg_v[...], cos_s[...], sin_s[...])
    local[4].wait()
    fresh_s[1] = jnp.dot(modded[...], w_v[2], preferred_element_type=jnp.float32).astype(
        jnp.bfloat16
    )
    local[5].wait()
    local[7].wait()
    img_at = pl.ds(txt_rows, img_rows)
    proj[img_at, :] = jnp.dot(modded[img_at, :], w_v[0], preferred_element_type=jnp.float32)
    for hh in range(heads):
        at = pl.ds(hh * HD, HD)
        q_s[:, at] = rotated(proj[img_at, at], qg_v[...], cos_s[img_at, :], sin_s[img_at, :])

    exp_scale = HD ** (-0.5) * math.log2(math.e)

    def scores_of(hh, keys):
        return (
            lax.dot_general(
                q_s[:, pl.ds(hh * HD, HD)],
                keys,
                (((1,), (1,)), ((), ())),
                preferred_element_type=jnp.float32,
            )
            * exp_scale
        )

    for hh in range(heads):
        at = pl.ds(hh * HD, HD)
        scores = scores_of(hh, fresh_s[0, :, at])
        top = jnp.max(scores, axis=-1, keepdims=True)
        expo = jnp.exp2(scores - top)
        m_s[hh] = top
        l_s[hh] = jnp.sum(expo, axis=-1, keepdims=True)
        acc_s[hh] = jnp.dot(
            expo.astype(jnp.bfloat16), fresh_s[1, :, at], preferred_element_type=jnp.float32
        )

    w_landed(order[0])

    def f32(values):
        return values.astype(jnp.float32)

    for copy in local[8:]:
        copy.wait()
    channels = lat_v.shape[1]
    wf_v[pl.ds(channels, wf_v.shape[0] - channels), :] = jnp.zeros(
        (wf_v.shape[0] - channels, cols), jnp.bfloat16
    )
    scale_up = 1.0 + fmod_v[1:2, my_cols]
    shift_up = fmod_v[0:1, my_cols]
    lines = lax.broadcasted_iota(jnp.int32, (8, cols), 0)
    scale_hi, shift_hi = f32(scale_up.astype(jnp.bfloat16)), f32(shift_up.astype(jnp.bfloat16))
    rows_up = jnp.where(lines == 0, scale_hi, jnp.where(lines == 1, scale_up - scale_hi, 0.0))
    rows_up = jnp.where(lines == 2, shift_hi, jnp.where(lines == 3, shift_up - shift_hi, rows_up))

    def to_channels(values):
        return lax.dot_general(
            values, wf_v[...], (((1,), (1,)), ((), ())), preferred_element_type=jnp.float32
        )

    vec_s[...] = to_channels(rows_up.astype(jnp.bfloat16))

    def each_owner(act):
        for dc, dh in owners:
            to_cfg, to_head = lax.rem(cfg + dc, 2), lax.rem(head + dh, 4)
            wanted = is_mid | (to_cfg == side)
            slot = to_cfg * 4 + to_head
            where_to = {"cfg": to_cfg, "head": to_head}
            at = dc * 4 + dh

            @pl.when(wanted)
            def _():
                act(at, slot, where_to, dc == 0 and dh == 0)

    def vec_copy(at, where_to):
        return remote(
            vec_s, vec_in.at[cfg, third], u_send.at[at], u_recv.at[cfg, third], where_to
        )

    def vel_copy(at, slot, where_to):
        return remote(
            vel_s.at[slot], vel_in.at[cfg, third], v_send.at[at], v_recv.at[cfg, third], where_to
        )

    def vec_start(at, slot, where_to, mine):
        if mine:
            vec_in[cfg, third] = vec_s[...]
        else:
            vec_copy(at, where_to).start()

    each_owner(vec_start)

    def attn_full(r, hh):
        return remote(
            attn_s.at[hh], attn_in.at[r, hh], at_send.at[r, hh], at_recv.at[r, hh],
            {"head": partners[r]},
        )

    def attn_half(hh):
        return remote(
            attn_s.at[hh, half_at], attn_in.at[0, hh, half_at], at_send.at[0, hh],
            at_recv.at[0, hh], {"head": mate},
        )

    def attn_relay(r, hh):
        return remote(
            attn_in.at[r, hh, half_at], attn_in.at[3 - r, hh, half_at], fw_send.at[r - 1, hh],
            at_recv.at[3 - r, hh], {"head": mate},
        )

    def other_block(j, hh):
        scores = scores_of(hh, kv_s[j, 0, hh])
        old = m_s[hh]
        top = jnp.maximum(old, jnp.max(scores, axis=-1, keepdims=True))
        factor = jnp.exp2(old - top)
        expo = jnp.exp2(scores - top)
        m_s[hh] = top
        l_s[hh] = l_s[hh] * factor + jnp.sum(expo, axis=-1, keepdims=True)
        acc_s[hh] = acc_s[hh] * factor + jnp.dot(
            expo.astype(jnp.bfloat16), kv_s[j, 1, hh], preferred_element_type=jnp.float32
        )

    for hh in range(heads):
        for j in range(1, n_patch):
            for which in range(2):
                kv_copy(j, hh, which).wait_recv()
        if n_patch <= 2:
            for j in range(n_patch - 1):
                other_block(j, hh)
        else:
            lax.fori_loop(0, n_patch - 1, lambda j, c: (other_block(j, hh), c)[1], 0)
        attn_s[hh] = (acc_s[hh] / l_s[hh]).astype(jnp.bfloat16)

        @pl.when(is_end)
        def _():
            attn_full(2, hh).start()
            attn_full(0, hh).start()

        @pl.when(is_mid)
        def _():
            attn_full(1, hh).start()
            attn_half(hh).start()

        if hh < 2:
            w_landed(order[hh + 1])

    def joined(ref, at):
        return jnp.concatenate([ref[hh, at, :] for hh in range(heads)], axis=1)

    def project(ref, weights, at):
        return jnp.dot(joined(ref, at), weights, preferred_element_type=jnp.float32)

    everything = pl.ds(0, img_rows)

    def on_rows(act):
        @pl.when(is_mid)
        def _():
            act(everything, img_rows)

        @pl.when(is_end)
        def _():
            act(half_at, half)

    def start_acc(at, count):
        out_acc[at, :] = project(attn_s, wo_v[...], at)

    on_rows(start_acc)

    for r in order:
        w_over_y(r, 0).wait_recv()
        w_over_c(r, 2).start()
    for hh, r in enumerate(order):
        w_over_x(r).wait_recv()
        w_over_y(r, 1).start()
        w_over_c(r, 1).start()

        @pl.when(is_mid)
        def _():
            for s in (1, 2):
                attn_full(s, hh).wait_recv()
                attn_relay(s, hh).start()

    for r in order:
        w_over_y(r, 1).wait_recv()
        w_over_c(r, 3).start()

    @pl.when(is_mid)
    def _():
        for hh in range(heads):
            attn_full(0, hh).wait_recv()

    @pl.when(is_end)
    def _():
        for hh in range(heads):
            attn_half(hh).wait_recv()
            for s in (1, 2):
                attn_relay(3 - s, hh).wait_recv()

    for r in order:
        for k in range(4):
            w_over_c(r, k).wait_recv()

        def add_acc(at, count):
            out_acc[at, :] += project(attn_in.at[r], w_in[r], at)

        on_rows(add_acc)

    gate = mod_v[2, :, my_cols]
    bias = bo_v[:, my_cols]
    lanes = lax.broadcasted_iota(jnp.int32, (LN_ROWS, HD), 1)

    def final_step(first):
        def run(i, carry):
            at = pl.ds(pl.multiple_of(first + i * LN_ROWS, LN_ROWS), LN_ROWS)
            mixed = f32(hid_v[at, my_cols]) + gate * (out_acc[at, :] + bias)
            mean = jnp.mean(mixed, axis=-1, keepdims=True)
            centered = mixed - mean
            spread = jnp.sum(centered * centered, axis=-1, keepdims=True)
            scaled = centered * scale_up
            high = scaled.astype(jnp.bfloat16)
            hi_s[at, :] = high
            lo_s[at, :] = (scaled - f32(high)).astype(jnp.bfloat16)
            stat_s[at, :] = jnp.where(
                lanes == channels, mean, jnp.where(lanes == channels + 1, spread, 0.0)
            )
            return carry

        return run

    def finish(at, count):
        first = 0 if count == img_rows else side * half
        lax.fori_loop(0, count // LN_ROWS, final_step(first), 0, unroll=LN_UNROLL)
        value = to_channels(hi_s[at, :]) + to_channels(lo_s[at, :]) + stat_s[at, :]
        for i in range(count // out_rows):
            slot = i if count == img_rows else side * 4 + i
            vel_s[slot] = value[i * out_rows : (i + 1) * out_rows]

    on_rows(finish)

    def vel_start(at, slot, where_to, mine):
        if mine:
            vel_in[cfg, third] = vel_s[slot]
        else:
            vel_copy(at, slot, where_to).start()

    each_owner(vel_start)

    ones = jnp.ones(lat_v.shape, jnp.float32)
    index = ones * step_index[0].astype(jnp.float32)
    count = ones * step_count[0].astype(jnp.float32)
    sigma_prev = noise_level(index - 1.0, count)
    sigma_now = noise_level(index, count)
    sigma_next = noise_level(index + 1.0, count)
    step_now = log_ratio(sigma_next) - log_ratio(sigma_now)
    step_prev = log_ratio(sigma_now) - log_ratio(sigma_prev)
    ratio = step_prev / step_now
    shrink = (1.0 - sigma_next) * (jnp.exp(-step_now) - 1.0)
    latent = lat_v[...]

    for b in range(2):
        for k in range(THIRDS):
            source = 3 * cfg if k == 0 else k

            @pl.when((cfg != b) | (head != source))
            def _():
                where_to = {"cfg": cfg, "head": head}
                for kind in (0, 1):
                    pltpu.make_async_remote_copy(
                        src_ref=vec_s if kind else vel_s.at[0],
                        dst_ref=vec_in.at[b, k] if kind else vel_in.at[b, k],
                        send_sem=u_send.at[0] if kind else v_send.at[0],
                        recv_sem=u_recv.at[b, k] if kind else v_recv.at[b, k],
                        device_id=c_dev,
                        device_id_type=MESH,
                    ).wait_recv()

    def velocity(b):
        means = [vel_in[b, k, :, channels : channels + 1] for k in range(THIRDS)]
        mean = sum(means) / THIRDS
        spread = sum(vel_in[b, k, :, channels + 1 : channels + 2] for k in range(THIRDS))
        spread = spread + cols * sum((m - mean) * (m - mean) for m in means)
        total = 0.0
        base = bf_v[...]
        for k in range(THIRDS):
            lift = vec_in[b, k, 0:1, :channels] + vec_in[b, k, 1:2, :channels]
            base = base + vec_in[b, k, 2:3, :channels] + vec_in[b, k, 3:4, :channels]
            total = total + vel_in[b, k, :, :channels] + (means[k] - mean) * lift
        return total * lax.rsqrt(spread / d + epsilon) + base

    cond, uncond = velocity(0), velocity(1)
    guided = uncond + guidance[0] * (cond - uncond)
    denoised = latent - sigma_now * guided
    blend = (1.0 + 0.5 / ratio) * denoised - 0.5 / ratio * prev_v[...]
    step_o[1] = denoised
    step_o[0] = sigma_next / sigma_now * latent - shrink * blend

    for hh in range(heads):
        for which in range(2):
            for j in range(1, n_patch):
                kv_copy(j, hh, which).wait_send()
    for r in order:
        w_over_z(r).wait_send()
        w_over_x(r).wait_send()
        for k in range(2):
            w_over_y(r, k).wait_send()
        for k in range(4):
            w_over_c(r, k).wait_send()

    @pl.when(is_end)
    def _():
        for hh in range(heads):
            attn_full(0, hh).wait_send()
            attn_full(2, hh).wait_send()

    @pl.when(is_mid)
    def _():
        for hh in range(heads):
            attn_full(1, hh).wait_send()
            attn_half(hh).wait_send()
            for s in (1, 2):
                attn_relay(s, hh).wait_send()

    def sent(at, slot, where_to, mine):
        if not mine:
            vec_copy(at, where_to).wait_send()
            vel_copy(at, slot, where_to).wait_send()

    each_owner(sent)


def deliver(fresh, stepped, fresh_o, next_o, den_o, fresh_v, step_v, in_sem, out_sem):
    loads = [
        pltpu.make_async_copy(stepped, step_v, in_sem.at[0]),
        pltpu.make_async_copy(fresh, fresh_v, in_sem.at[1]),
    ]
    for copy in loads:
        copy.start()
    pairs = ((step_v.at[0], next_o), (step_v.at[1], den_o), (fresh_v, fresh_o))
    stores = [pltpu.make_async_copy(s, t, out_sem.at[i]) for i, (s, t) in enumerate(pairs)]
    loads[0].wait()
    stores[0].start()
    stores[1].start()
    loads[1].wait()
    stores[2].start()
    for copy in stores:
        copy.wait()


def body(
    n_patch,
    img_hidden, txt_hidden, modulation, w_qkv, q_gain, k_gain, w_out, b_out, stale_kv,
    final_mod, w_final, b_final, latent, prev_denoised, guidance, step_index, step_count,
):
    bf16, f32 = jnp.bfloat16, jnp.float32
    img_rows, d = img_hidden.shape[1:]
    txt_rows = txt_hidden.shape[1]
    kv_rows = img_rows + txt_rows
    head_width = w_out.shape[0]
    heads = head_width // HD
    out_rows, channels = latent.shape
    cols = d // THIRDS
    args = (
        img_hidden[0],
        txt_hidden[0],
        modulation.transpose(1, 0, 2),
        w_qkv.transpose(1, 0, 2),
        q_gain[None],
        k_gain[None],
        w_out,
        b_out[None],
        stale_kv[0],
        final_mod[0],
        w_final.T,
        b_final[None],
        latent,
        prev_denoised,
    )
    dma = pltpu.SemaphoreType.DMA
    shapes = {6: (head_width, cols), 10: (HD, cols)}
    remotes = n_patch - 1
    scratch = [
        pltpu.VMEM(shapes.get(i, a.shape), a.dtype) for i, a in enumerate(args) if i != 8
    ] + [
        pltpu.VMEM((kv_rows, d), bf16),
        pltpu.VMEM((kv_rows, head_width), f32),
        pltpu.VMEM((kv_rows, HD), f32),
        pltpu.VMEM((kv_rows, HD), f32),
        pltpu.VMEM((img_rows, head_width), bf16),
        pltpu.VMEM((remotes, 2, heads, kv_rows, HD), bf16),
        pltpu.VMEM((heads, img_rows, 1), f32),
        pltpu.VMEM((heads, img_rows, 1), f32),
        pltpu.VMEM((heads, img_rows, HD), f32),
        pltpu.VMEM((heads, img_rows, HD), bf16),
        pltpu.VMEM((3, heads, img_rows, HD), bf16),
        pltpu.VMEM((3, head_width, cols), bf16),
        pltpu.VMEM((img_rows, cols), f32),
        pltpu.VMEM((img_rows, cols), bf16),
        pltpu.VMEM((img_rows, cols), bf16),
        pltpu.VMEM((img_rows, HD), f32),
        pltpu.VMEM((PLANE, out_rows, HD), f32),
        pltpu.VMEM((2, THIRDS, out_rows, HD), f32),
        pltpu.VMEM((8, HD), f32),
        pltpu.VMEM((2, THIRDS, 8, HD), f32),
        dma((15,)),
        dma((remotes, 2, heads)),
        dma((remotes, 2, heads)),
        dma((3,)),
        dma((3,)),
        dma((3,)),
        dma((3,)),
        dma((3, 2)),
        dma((3, 2)),
        dma((3, 4)),
        dma((3, 4)),
        dma((3, heads)),
        dma((3, heads)),
        dma((2, heads)),
        dma((PLANE,)),
        dma((2, THIRDS)),
        dma((PLANE,)),
        dma((2, THIRDS)),
    ]
    vmem = pl.BlockSpec(memory_space=pltpu.VMEM)
    smem = pl.BlockSpec(memory_space=pltpu.SMEM)
    anywhere = pl.BlockSpec(memory_space=pl.ANY)
    fresh, stepped = pl.pallas_call(
        functools.partial(kernel, n_patch),
        out_shape=(
            jax.ShapeDtypeStruct((2, kv_rows, head_width), bf16),
            jax.ShapeDtypeStruct((2, out_rows, channels), f32),
        ),
        in_specs=[anywhere] * len(args) + [smem] * 3,
        out_specs=(vmem, vmem),
        scratch_shapes=scratch,
        compiler_params=pltpu.CompilerParams(
            collective_id=0, has_side_effects=True, vmem_limit_bytes=VMEM_MAIN
        ),
    )(*args, guidance, step_index, step_count)
    fresh, next_latent, denoised = pl.pallas_call(
        deliver,
        out_shape=(
            jax.ShapeDtypeStruct(fresh.shape, bf16),
            jax.ShapeDtypeStruct(latent.shape, f32),
            jax.ShapeDtypeStruct(latent.shape, f32),
        ),
        in_specs=[anywhere, anywhere],
        out_specs=(anywhere, anywhere, anywhere),
        scratch_shapes=[
            pltpu.VMEM(fresh.shape, bf16),
            pltpu.VMEM(stepped.shape, f32),
            dma((2,)),
            dma((3,)),
        ],
        compiler_params=pltpu.CompilerParams(vmem_limit_bytes=VMEM_MAIN),
    )(fresh, stepped)
    return fresh[None], next_latent, denoised


def solution(mesh):
    return jax.shard_map(
        functools.partial(body, mesh.shape["patch"]),
        mesh=mesh,
        in_specs=(
            P("cfg", ("groups", "patch"), None),
            P("cfg", ("groups", "patch"), None),
            P(("groups", "cfg"), None, None),
            P(None, None, "head"),
            P(),
            P(),
            P("head", None),
            P(),
            P("cfg", None, ("groups", "patch"), "head"),
            P(("groups", "cfg"), None, None),
            P(),
            P(),
            P(("groups", "patch", "cfg", "head"), None),
            P(("groups", "patch", "cfg", "head"), None),
            P("groups"),
            P(),
            P(),
        ),
        out_specs=(
            P("cfg", None, ("groups", "patch"), "head"),
            P(("groups", "patch", "cfg", "head"), None),
            P(("groups", "patch", "cfg", "head"), None),
        ),
        check_vma=False,
    )
```

time: 51 us -> 41.5 us (0.81)
  Pallas kernels: 48.1 us -> 38.4 us
    pallas_call x1, Pallas kernels: 46.3 us -> 36.6 us  [body(): pl.pallas_call(functools.partial(kernel, n_patch), out_shape=(jax.ShapeDt...]
where the time goes in v1:
time: 41.5 us; the launch traced here: 41 us
  Pallas kernels  38.4 us (93%)
  between operations  2.58 us (6%)
    pallas_call x1, Pallas kernels, body(): pl.pallas_call(functools.partial(kernel, n_patch), out_shape=(jax.ShapeDt...  36.6 us
    pallas_call x1, Pallas kernels, body(): pl.pallas_call(deliver, out_shape=(jax.ShapeDtypeStruct(fresh.shape, bf16...  1.82 us

profile of v1, /device:TPU:1, one launch (start us, length us, event | category | flops | bytes accessed | tf_op | source)
XLA Modules:
  0.0 41.0 jit_solution(6186920854870234448)
XLA Ops:
  2.6 36.6 %shard_map.184 = (bf16[2,272,384]{2,1,0:T(8,128)(2,1)}, f32[2,32,64]{2,1,0:T(8,128)}) custom-call(bf16[256,3072]{1,0:T(8,128)(2,1)} %bitcast.13, bf16[16,3072]{1,0:T(8,128)(2,1)} %bitcast.16, f32[3,1,3072]{2,1,0:T(1,128)} %bitcast.17, bf16[3,3072,384]{2,1,0:T(8,128)(2,1)} %bitcast.12, f32[1,128]{1,0:T(1,128)} %bitcast.20, f32[1,128]{1,0:T(1,128)} %bitcast.21, ...), custom_call_target="tpu_custom_call" | custom-call | tf_op jit(solution)/shard_map/pallas_call | solution.py:624
  39.2 1.8 %shard_map.185 = (bf16[2,272,384]{2,1,0:T(8,128)(2,1)}, f32[32,64]{1,0:T(8,128)}, f32[32,64]{1,0:T(8,128)}) custom-call(bf16[2,272,384]{2,1,0:T(8,128)(2,1)} %get-tuple-element.8.fresh, f32[2,32,64]{2,1,0:T(8,128)} %get-tuple-element.9.stepped), custom_call_target="tpu_custom_call" | custom-call | tf_op jit(solution)/shard_map/pallas_call | solution.py:637

commit v2 on v1

--- a/solution.py
+++ b/solution.py
@@ -68,9 +68,9 @@
     hid, txt, mod, w_qkv, q_gain, k_gain, w_out, b_out, stale, fmod, w_fin, b_fin, lat, prev,
     guidance, step_index, step_count,
     fresh_s, step_o,
-    hid_v, txt_v, mod_v, w_v, qg_v, kg_v, wo_v, bo_v, fmod_v, wf_v, bf_v, lat_v, prev_v,
+    stale_v, pair_v, hid_v, txt_v, mod_v, w_v, qg_v, kg_v, wo_v, bo_v, fmod_v, wf_v, bf_v, lat_v, prev_v,
     modded, proj, cos_s, sin_s, q_s, kv_s, m_s, l_s, acc_s, attn_s, attn_in,
-    w_in, out_acc, hi_s, lo_s, stat_s, vel_s, vel_in, vec_s, vec_in,
+    w_in, base_s, out_acc, hi_s, lo_s, stat_s, vel_s, vel_in, vec_s, vec_in,
     loc_sem, kv_send, kv_recv, wz_send, wz_recv, wx_send, wx_recv, wy_send, wy_recv,
     wc_send, wc_recv, at_send, at_recv, fw_send, v_send, v_recv, u_send, u_recv,
 ):
@@ -99,6 +99,8 @@
     my_cols = pl.ds(pl.multiple_of(third * cols, HD), cols)
     half_at = pl.ds(pl.multiple_of(side * half, half), half)
 
+    pair_at = pl.ds(pl.multiple_of((cfg * 2 + group) * 2 * share, 16), 2 * share)
+    first_pairs = [(stale, stale_v), (w_out.at[pair_at], pair_v)]
     pairs = [
         (mod, mod_v), (txt, txt_v), (hid, hid_v),
         (w_qkv.at[1], w_v.at[1]), (w_qkv.at[2], w_v.at[2]), (w_qkv.at[0], w_v.at[0]),
@@ -106,9 +108,12 @@
         (fmod, fmod_v), (w_fin.at[:, my_cols], wf_v.at[pl.ds(0, w_fin.shape[0])]),
         (b_fin, bf_v), (lat, lat_v), (prev, prev_v),
     ]
-    local = [pltpu.make_async_copy(s, t, loc_sem.at[i]) for i, (s, t) in enumerate(pairs)]
-    for copy in local:
+    loads = [
+        pltpu.make_async_copy(s, t, loc_sem.at[i]) for i, (s, t) in enumerate(first_pairs + pairs)
+    ]
+    for copy in loads:
         copy.start()
+    local = loads[2:]
 
     def remote(source, target, send, recv, device):
         return pltpu.make_async_remote_copy(
@@ -124,11 +129,13 @@
     for peer in peers:
         pl.semaphore_signal(barrier, inc=1, device_id=peer, device_id_type=MESH)
     rotation_tables(cos_s, sin_s, txt_rows, patch * img_rows)
+    loads[0].wait()
+    loads[1].wait()
     pl.semaphore_wait(barrier, len(peers))
 
     def kv_copy(j, hh, which):
         return remote(
-            stale.at[which, :, pl.ds(hh * HD, HD)], kv_s.at[j - 1, which, hh],
+            stale_v.at[which, :, pl.ds(hh * HD, HD)], kv_s.at[j - 1, which, hh],
             kv_send.at[j - 1, which, hh], kv_recv.at[j - 1, which, hh],
             {"patch": lax.rem(patch + j, n_patch)},
         )
@@ -146,34 +153,58 @@
 
     own = unit(0, 0, 0)
 
-    def w_over_z(r):
-        to = partners[r]
+    near = jnp.where(is_mid, 1, 2)
+    slots = (0, near, 3 - near)
+
+    def w_over_z(i, k=0):
+        r, rows = slots[i], unit(k, 0, 0)
+        to = mate if i == 0 else jnp.where(r == 1, partners[1], partners[2])
         at = pl.ds(pl.multiple_of(lax.rem(to, THIRDS) * cols, HD), cols)
+        bit = 1 - x_bit if k else x_bit
+        source = pl.ds(pl.multiple_of(bit * share, 16), share)
         return remote(
-            w_out.at[own, at], w_in.at[r, own], wz_send.at[r], wz_recv.at[r], {"head": to}
-        )
-
-    def w_over_x(r):
-        at = w_in.at[r, own]
-        return remote(at, at, wx_send.at[r], wx_recv.at[r], x_dev)
-
-    def w_over_y(r, k):
+            pair_v.at[source, at], w_in.at[r, rows], wz_send.at[r, k], wz_recv.at[r, k], {"head": to}
+        )
+
+    def w_over_x(i, k):
+        r = slots[i]
+        at = w_in.at[r, unit(0, k, 0)]
+        return remote(at, at, wx_send.at[r, k], wx_recv.at[r, k], x_dev)
+
+    def w_over_y(i, k):
+        r = slots[i]
         at = w_in.at[r, unit(k, 0, 0)]
         return remote(at, at, wy_send.at[r, k], wy_recv.at[r, k], y_dev)
 
-    def w_over_c(r, k):
+    def w_over_c(i, k):
+        r = slots[i]
         at = w_in.at[r, unit(k % 2, k // 2, 0)]
         return remote(at, at, wc_send.at[r, k], wc_recv.at[r, k], c_dev)
 
-    order = (0, 2, 1)
-    for r in order:
-        w_over_z(r).start()
-
-    def w_landed(r):
-        w_over_z(r).wait_recv()
-        w_over_x(r).start()
-        w_over_y(r, 0).start()
-        w_over_c(r, 0).start()
+    z_units = ((0, 0), (1, 0), (2, 0), (0, 1))
+    x_units = ((1, 0), (2, 0), (2, 1))
+    y_units = ((0, 0), (1, 0), (2, 0), (0, 1), (1, 1))
+    for i, k in z_units:
+        w_over_z(i, k).start()
+
+    def w_landed(i, k=0):
+        w_over_z(i, k).wait_recv()
+        if i:
+            w_over_x(i, 0).start()
+        w_over_y(i, k).start()
+        w_over_c(i, k).start()
+
+    def w_crossed(i, k=0):
+        w_over_x(i, k).wait_recv()
+        if i == 1:
+            w_over_y(1, 1).start()
+        w_over_c(i, 1 + 2 * k).start()
+
+    def w_passed(i, k):
+        w_over_y(i, k).wait_recv()
+        if i == 2:
+            w_over_x(2, 1).start()
+        w_over_c(i, 2 + k).start()
 
     for copy in local[:3]:
         copy.wait()
@@ -209,6 +240,7 @@
         at = pl.ds(hh * HD, HD)
         q_s[:, at] = rotated(proj[img_at, at], qg_v[...], cos_s[img_at, :], sin_s[img_at, :])
 
+    w_landed(0)
     exp_scale = HD ** (-0.5) * math.log2(math.e)
 
     def scores_of(hh, keys):
@@ -232,8 +264,6 @@
         acc_s[hh] = jnp.dot(
             expo.astype(jnp.bfloat16), fresh_s[1, :, at], preferred_element_type=jnp.float32
         )
-
-    w_landed(order[0])
 
     def f32(values):
         return values.astype(jnp.float32)
@@ -339,8 +369,12 @@
             attn_full(1, hh).start()
             attn_half(hh).start()
 
-        if hh < 2:
-            w_landed(order[hh + 1])
+        if hh == 0:
+            w_landed(1)
+        if hh == heads - 2:
+            w_landed(2)
+
+    w_landed(0, 1)
 
     def joined(ref, at):
         return jnp.concatenate([ref[hh, at, :] for hh in range(heads)], axis=1)
@@ -362,55 +396,68 @@
     def start_acc(at, count):
         out_acc[at, :] = project(attn_s, wo_v[...], at)
 
+    gate = mod_v[2, :, my_cols]
+    bias = bo_v[:, my_cols]
+
+    def residual(at, count):
+        base_s[at, :] = f32(hid_v[at, my_cols]) + gate * bias
+
+    w_passed(0, 0)
+    w_passed(1, 0)
     on_rows(start_acc)
-
-    for r in order:
-        w_over_y(r, 0).wait_recv()
-        w_over_c(r, 2).start()
-    for hh, r in enumerate(order):
-        w_over_x(r).wait_recv()
-        w_over_y(r, 1).start()
-        w_over_c(r, 1).start()
-
+    on_rows(residual)
+
+    def pass_on(hh):
         @pl.when(is_mid)
         def _():
-            for s in (1, 2):
-                attn_full(s, hh).wait_recv()
-                attn_relay(s, hh).start()
-
-    for r in order:
-        w_over_y(r, 1).wait_recv()
-        w_over_c(r, 3).start()
-
-    @pl.when(is_mid)
-    def _():
-        for hh in range(heads):
-            attn_full(0, hh).wait_recv()
-
-    @pl.when(is_end)
-    def _():
-        for hh in range(heads):
-            attn_half(hh).wait_recv()
-            for s in (1, 2):
-                attn_relay(3 - s, hh).wait_recv()
-
-    for r in order:
+            for r in (1, 2):
+                attn_full(r, hh).wait_recv()
+                attn_relay(r, hh).start()
+
+    def add_head(i):
         for k in range(4):
-            w_over_c(r, k).wait_recv()
+            w_over_c(i, k).wait_recv()
+        r = slots[i]
+
+        @pl.when(is_end)
+        def _():
+            for hh in range(heads):
+                if i == 0:
+                    attn_half(hh).wait_recv()
+                else:
+                    attn_relay(i, hh).wait_recv()
+
+        @pl.when(is_mid)
+        def _():
+            if i == 0:
+                for hh in range(heads):
+                    attn_full(0, hh).wait_recv()
 
         def add_acc(at, count):
             out_acc[at, :] += project(attn_in.at[r], w_in[r], at)
 
         on_rows(add_acc)
 
-    gate = mod_v[2, :, my_cols]
-    bias = bo_v[:, my_cols]
+    pass_on(0)
+    w_crossed(1)
+    w_passed(2, 0)
+    for hh in range(1, heads - 1):
+        pass_on(hh)
+    w_crossed(2)
+    w_passed(0, 1)
+    w_crossed(2, 1)
+    w_passed(1, 1)
+    pass_on(heads - 1)
+    add_head(0)
+    add_head(1)
+    add_head(2)
+
     lanes = lax.broadcasted_iota(jnp.int32, (LN_ROWS, HD), 1)
 
     def final_step(first):
         def run(i, carry):
             at = pl.ds(pl.multiple_of(first + i * LN_ROWS, LN_ROWS), LN_ROWS)
-            mixed = f32(hid_v[at, my_cols]) + gate * (out_acc[at, :] + bias)
+            mixed = base_s[at, :] + gate * out_acc[at, :]
             mean = jnp.mean(mixed, axis=-1, keepdims=True)
             centered = mixed - mean
             spread = jnp.sum(centered * centered, axis=-1, keepdims=True)
@@ -418,9 +465,11 @@
             high = scaled.astype(jnp.bfloat16)
             hi_s[at, :] = high
             lo_s[at, :] = (scaled - f32(high)).astype(jnp.bfloat16)
-            stat_s[at, :] = jnp.where(
-                lanes == channels, mean, jnp.where(lanes == channels + 1, spread, 0.0)
-            )
+            mean_hi, spread_hi = f32(mean.astype(jnp.bfloat16)), f32(spread.astype(jnp.bfloat16))
+            stat = jnp.where(lanes == channels, mean_hi, 0.0)
+            stat = jnp.where(lanes == channels + 1, mean - mean_hi, stat)
+            stat = jnp.where(lanes == channels + 2, spread_hi, stat)
+            stat_s[at, :] = jnp.where(lanes == channels + 3, spread - spread_hi, stat)
             return carry
 
         return run
@@ -431,7 +480,7 @@
         value = to_channels(hi_s[at, :]) + to_channels(lo_s[at, :]) + stat_s[at, :]
         for i in range(count // out_rows):
             slot = i if count == img_rows else side * 4 + i
-            vel_s[slot] = value[i * out_rows : (i + 1) * out_rows]
+            vel_s[slot] = value[i * out_rows : (i + 1) * out_rows].astype(jnp.bfloat16)
 
     on_rows(finish)
 
@@ -473,16 +522,21 @@
                     ).wait_recv()
 
     def velocity(b):
-        means = [vel_in[b, k, :, channels : channels + 1] for k in range(THIRDS)]
+        parts = [f32(vel_in[b, k]) for k in range(THIRDS)]
+
+        def stat_of(part, lane):
+            return part[:, lane : lane + 1] + part[:, lane + 1 : lane + 2]
+
+        means = [stat_of(part, channels) for part in parts]
         mean = sum(means) / THIRDS
-        spread = sum(vel_in[b, k, :, channels + 1 : channels + 2] for k in range(THIRDS))
+        spread = sum(stat_of(part, channels + 2) for part in parts)
         spread = spread + cols * sum((m - mean) * (m - mean) for m in means)
         total = 0.0
         base = bf_v[...]
         for k in range(THIRDS):
             lift = vec_in[b, k, 0:1, :channels] + vec_in[b, k, 1:2, :channels]
             base = base + vec_in[b, k, 2:3, :channels] + vec_in[b, k, 3:4, :channels]
-            total = total + vel_in[b, k, :, :channels] + (means[k] - mean) * lift
+            total = total + parts[k][:, :channels] + (means[k] - mean) * lift
         return total * lax.rsqrt(spread / d + epsilon) + base
 
     cond, uncond = velocity(0), velocity(1)
@@ -496,13 +550,15 @@
         for which in range(2):
             for j in range(1, n_patch):
                 kv_copy(j, hh, which).wait_send()
-    for r in order:
-        w_over_z(r).wait_send()
-        w_over_x(r).wait_send()
-        for k in range(2):
-            w_over_y(r, k).wait_send()
+    for i, k in z_units:
+        w_over_z(i, k).wait_send()
+    for i, k in x_units:
+        w_over_x(i, k).wait_send()
+    for i, k in y_units:
+        w_over_y(i, k).wait_send()
+    for i in range(3):
         for k in range(4):
-            w_over_c(r, k).wait_send()
+            w_over_c(i, k).wait_send()
 
     @pl.when(is_end)
     def _():
@@ -577,6 +633,9 @@
     shapes = {6: (head_width, cols), 10: (HD, cols)}
     remotes = n_patch - 1
     scratch = [
+        pltpu.VMEM((2, kv_rows, head_width), bf16),
+        pltpu.VMEM((2 * head_width // PLANE, d), bf16),
+    ] + [
         pltpu.VMEM(shapes.get(i, a.shape), a.dtype) for i, a in enumerate(args) if i != 8
     ] + [
         pltpu.VMEM((kv_rows, d), bf16),
@@ -592,20 +651,21 @@
         pltpu.VMEM((3, heads, img_rows, HD), bf16),
         pltpu.VMEM((3, head_width, cols), bf16),
         pltpu.VMEM((img_rows, cols), f32),
+        pltpu.VMEM((img_rows, cols), f32),
         pltpu.VMEM((img_rows, cols), bf16),
         pltpu.VMEM((img_rows, cols), bf16),
         pltpu.VMEM((img_rows, HD), f32),
-        pltpu.VMEM((PLANE, out_rows, HD), f32),
-        pltpu.VMEM((2, THIRDS, out_rows, HD), f32),
+        pltpu.VMEM((PLANE, out_rows, HD), bf16),
+        pltpu.VMEM((2, THIRDS, out_rows, HD), bf16),
         pltpu.VMEM((8, HD), f32),
         pltpu.VMEM((2, THIRDS, 8, HD), f32),
-        dma((15,)),
+        dma((17,)),
         dma((remotes, 2, heads)),
         dma((remotes, 2, heads)),
-        dma((3,)),
-        dma((3,)),
-        dma((3,)),
-        dma((3,)),
+        dma((3, 2)),
+        dma((3, 2)),
+        dma((3, 2)),
+        dma((3, 2)),
         dma((3, 2)),
         dma((3, 2)),
         dma((3, 4)),

time: 41.5 us -> 39.6 us (0.954)
  Pallas kernels: 38.4 us -> 36.9 us
    pallas_call x1, Pallas kernels: 36.6 us -> 35.1 us  [body(): pl.pallas_call(functools.partial(kernel, n_patch), out_shape=(jax.ShapeDt...]
where the time goes in v2:
time: 39.6 us; the launch traced here: 39.5 us
  Pallas kernels  36.9 us (93%)
  between operations  2.58 us (7%)
    pallas_call x1, Pallas kernels, body(): pl.pallas_call(functools.partial(kernel, n_patch), out_shape=(jax.ShapeDt...  35.1 us
    pallas_call x1, Pallas kernels, body(): pl.pallas_call(deliver, out_shape=(jax.ShapeDtypeStruct(fresh.shape, bf16...  1.82 us

profile of v2, /device:TPU:1, one launch (start us, length us, event | category | flops | bytes accessed | tf_op | source)
XLA Modules:
  0.0 39.5 jit_solution(18347403900000749173)
XLA Ops:
  2.6 35.1 %shard_map.184 = (bf16[2,272,384]{2,1,0:T(8,128)(2,1)}, f32[2,32,64]{2,1,0:T(8,128)}) custom-call(bf16[256,3072]{1,0:T(8,128)(2,1)} %bitcast.13, bf16[16,3072]{1,0:T(8,128)(2,1)} %bitcast.16, f32[3,1,3072]{2,1,0:T(1,128)} %bitcast.17, bf16[3,3072,384]{2,1,0:T(8,128)(2,1)} %bitcast.12, f32[1,128]{1,0:T(1,128)} %bitcast.20, f32[1,128]{1,0:T(1,128)} %bitcast.21, ...), custom_call_target="tpu_custom_call" | custom-call | tf_op jit(solution)/shard_map/pallas_call | solution.py:684
  37.6 1.8 %shard_map.185 = (bf16[2,272,384]{2,1,0:T(8,128)(2,1)}, f32[32,64]{1,0:T(8,128)}, f32[32,64]{1,0:T(8,128)}) custom-call(bf16[2,272,384]{2,1,0:T(8,128)(2,1)} %get-tuple-element.8.fresh, f32[2,32,64]{2,1,0:T(8,128)} %get-tuple-element.9.stepped), custom_call_target="tpu_custom_call" | custom-call | tf_op jit(solution)/shard_map/pallas_call | solution.py:697

commit v3 on v2

--- a/solution.py
+++ b/solution.py
@@ -14,7 +14,8 @@
 LN_UNROLL = 4
 THIRDS = 3
 PLANE = 8
-VMEM_MAIN = 67043328
+VMEM_MAIN = 41943040
+VMEM_DELIVER = 8388608
 
 epsilon = 1e-06
 time_shift = 3.0
@@ -582,20 +583,11 @@
     each_owner(sent)
 
 
-def deliver(fresh, stepped, fresh_o, next_o, den_o, fresh_v, step_v, in_sem, out_sem):
-    loads = [
-        pltpu.make_async_copy(stepped, step_v, in_sem.at[0]),
-        pltpu.make_async_copy(fresh, fresh_v, in_sem.at[1]),
-    ]
-    for copy in loads:
+def deliver(fresh, stepped, fresh_o, next_o, den_o, out_sem):
+    pairs = ((fresh, fresh_o), (stepped.at[0], next_o), (stepped.at[1], den_o))
+    stores = [pltpu.make_async_copy(s, t, out_sem.at[i]) for i, (s, t) in enumerate(pairs)]
+    for copy in stores:
         copy.start()
-    pairs = ((step_v.at[0], next_o), (step_v.at[1], den_o), (fresh_v, fresh_o))
-    stores = [pltpu.make_async_copy(s, t, out_sem.at[i]) for i, (s, t) in enumerate(pairs)]
-    loads[0].wait()
-    stores[0].start()
-    stores[1].start()
-    loads[1].wait()
-    stores[2].start()
     for copy in stores:
         copy.wait()
 
@@ -681,11 +673,12 @@
     vmem = pl.BlockSpec(memory_space=pltpu.VMEM)
     smem = pl.BlockSpec(memory_space=pltpu.SMEM)
     anywhere = pl.BlockSpec(memory_space=pl.ANY)
+    operands = [pltpu.with_memory_space_constraint(a, pltpu.HBM) for a in args]
     fresh, stepped = pl.pallas_call(
         functools.partial(kernel, n_patch),
         out_shape=(
-            jax.ShapeDtypeStruct((2, kv_rows, head_width), bf16),
-            jax.ShapeDtypeStruct((2, out_rows, channels), f32),
+            pltpu.VMEM((2, kv_rows, head_width), bf16),
+            pltpu.VMEM((2, out_rows, channels), f32),
         ),
         in_specs=[anywhere] * len(args) + [smem] * 3,
         out_specs=(vmem, vmem),
@@ -693,7 +686,7 @@
         compiler_params=pltpu.CompilerParams(
             collective_id=0, has_side_effects=True, vmem_limit_bytes=VMEM_MAIN
         ),
-    )(*args, guidance, step_index, step_count)
+    )(*operands, guidance, step_index, step_count)
     fresh, next_latent, denoised = pl.pallas_call(
         deliver,
         out_shape=(
@@ -701,15 +694,10 @@
             jax.ShapeDtypeStruct(latent.shape, f32),
             jax.ShapeDtypeStruct(latent.shape, f32),
         ),
-        in_specs=[anywhere, anywhere],
+        in_specs=[vmem, vmem],
         out_specs=(anywhere, anywhere, anywhere),
-        scratch_shapes=[
-            pltpu.VMEM(fresh.shape, bf16),
-            pltpu.VMEM(stepped.shape, f32),
-            dma((2,)),
-            dma((3,)),
-        ],
-        compiler_params=pltpu.CompilerParams(vmem_limit_bytes=VMEM_MAIN),
+        scratch_shapes=[dma((3,))],
+        compiler_params=pltpu.CompilerParams(vmem_limit_bytes=VMEM_DELIVER),
     )(fresh, stepped)
     return fresh[None], next_latent, denoised
 

time: 39.6 us -> 37.8 us (0.955)
  Pallas kernels: 36.9 us -> 35.1 us
    pallas_call x1, Pallas kernels: 1.82 us -> 0.79 us  [body(): pl.pallas_call(deliver, out_shape=(jax.ShapeDtypeStruct(fresh.shape, bf16...]
    pallas_call x1, Pallas kernels: 35.1 us -> 34.3 us  [body(): pl.pallas_call(functools.partial(kernel, n_patch), out_shape=(pltpu.VMEM(...]
where the time goes in v3:
time: 37.8 us; the launch traced here: 37.7 us
  Pallas kernels  35.1 us (93%)
  between operations  2.58 us (7%)
    pallas_call x1, Pallas kernels, body(): pl.pallas_call(functools.partial(kernel, n_patch), out_shape=(pltpu.VMEM(...  34.3 us
    pallas_call x1, Pallas kernels, body(): pl.pallas_call(deliver, out_shape=(jax.ShapeDtypeStruct(fresh.shape, bf16...  0.79 us

profile of v3, /device:TPU:1, one launch (start us, length us, event | category | flops | bytes accessed | tf_op | source)
XLA Modules:
  0.0 37.7 jit_solution(6803164771183569627)
XLA Ops:
  2.6 34.3 %shard_map.184 = (bf16[2,272,384]{2,1,0:T(8,128)(2,1)S(1)}, f32[2,32,64]{2,1,0:T(8,128)S(1)}) custom-call(bf16[256,3072]{1,0:T(8,128)(2,1)} %bitcast.13, bf16[16,3072]{1,0:T(8,128)(2,1)} %bitcast.16, f32[3,1,3072]{2,1,0:T(1,128)} %bitcast.17, bf16[3,3072,384]{2,1,0:T(8,128)(2,1)} %bitcast.12, f32[1,128]{1,0:T(1,128)} %bitcast.20, f32[1,128]{1,0:T(1,128)} %bitcast.21, ...), custom_call_target="tpu_custom_call" | custom-call | tf_op jit(solution)/shard_map/pallas_call | solution.py:677
  36.9 0.8 %shard_map.185 = (bf16[2,272,384]{2,1,0:T(8,128)(2,1)}, f32[32,64]{1,0:T(8,128)}, f32[32,64]{1,0:T(8,128)}) custom-call(bf16[2,272,384]{2,1,0:T(8,128)(2,1)S(1)} %get-tuple-element.8.fresh, f32[2,32,64]{2,1,0:T(8,128)S(1)} %get-tuple-element.9.stepped), custom_call_target="tpu_custom_call" | custom-call | tf_op jit(solution)/shard_map/pallas_call | solution.py:690
